TPU v7x, 16 devices: a 4x2x1 block of a 4x4x8 slice. The times are simulated.
16 devices in a mesh: dp: 2 (over y, z), tp: 8 (over x, core).
Axes of the slice: x: 4, y: 2, z: 1, core: 2. Of those that a mesh axis runs over, the one named last changes fastest.
The devices are a block of a 4x4x8 slice.
Arguments:
- hidden: bfloat16 [6, 3840], P('dp'), parts along dimension 0
- positions: int32 [6], P('dp'), parts along dimension 0
- k_local: bfloat16 [6, 1024, 8, 256], P('dp', None, 'tp'), parts along dimension 0
- v_local: bfloat16 [6, 1024, 8, 256], P('dp', None, 'tp'), parts along dimension 0
- k_global: bfloat16 [6, 6144, 8, 256], P('dp', None, 'tp'), parts along dimension 0
- v_global: bfloat16 [6, 6144, 8, 256], P('dp', None, 'tp'), parts along dimension 0
- w_query: bfloat16 [2, 3840, 4096], P(None, None, 'tp')
- w_key: bfloat16 [2, 3840, 2048], P(None, None, 'tp')
- w_value: bfloat16 [2, 3840, 2048], P(None, None, 'tp')
- w_out: bfloat16 [2, 4096, 3840], P(None, 'tp')
- w_gate: bfloat16 [2, 3840, 15360], P(None, None, 'tp')
- w_up: bfloat16 [2, 3840, 15360], P(None, None, 'tp')
- w_down: bfloat16 [2, 15360, 3840], P(None, 'tp')
- norm_scale: float32 [2, 4, 3840], replicated
Outputs:
- output 1: bfloat16 [6, 3840], P('dp'), parts along dimension 0
- output 2: bfloat16 [6, 1024, 8, 256], P('dp', None, 'tp'), parts along dimension 0
- output 3: bfloat16 [6, 1024, 8, 256], P('dp', None, 'tp'), parts along dimension 0
- output 4: bfloat16 [6, 6144, 8, 256], P('dp', None, 'tp'), parts along dimension 0
- output 5: bfloat16 [6, 6144, 8, 256], P('dp', None, 'tp'), parts along dimension 0
There are 2 independent parts. A program takes and returns all parts, laid end to end along the dimension named above; an argument that names none is the same for every part.
All inputs are finite; a program needn't handle non-finite values.
Results may differ from a plain program's by a relative error of at most 0.02.
Values are sent between devices in bfloat16 or wider.
A program may use at most 768 MiB of HBM per device.

v0:
```python
import jax
import jax.numpy as jnp
from jax import lax
from jax.sharding import PartitionSpec as P

SOFT_CAP = 50.0
NORM_EPS = 1e-6
ROPE_BASE = 10000.0
NEG_FILL = -1e30


def rms_norm(values, gain_row):
    values_f32 = values.astype(jnp.float32)
    inv_rms = lax.rsqrt(jnp.mean(values_f32 * values_f32, axis=-1, keepdims=True) + NORM_EPS)
    return (values_f32 * inv_rms * (1.0 + gain_row)).astype(jnp.bfloat16)


def rotary(projected, positions):
    head_dim = projected.shape[-1]
    half_dim = head_dim // 2
    inv_freq = ROPE_BASE ** (-2.0 * jnp.arange(half_dim, dtype=jnp.float32) / head_dim)
    angles = positions.astype(jnp.float32)[:, None, None] * inv_freq
    cos_part = jnp.cos(angles)
    sin_part = jnp.sin(angles)
    first_half = projected[..., :half_dim]
    second_half = projected[..., half_dim:]
    return jnp.concatenate([first_half * cos_part - second_half * sin_part, second_half * cos_part + first_half * sin_part], axis=-1)


def project_and_store(hidden, positions, k_cache, v_cache, slot_ids, w_query, w_key, w_value, gain_row):
    batch_rows = hidden.shape[0]
    kv_count = k_cache.shape[2]
    head_dim = k_cache.shape[3]
    normed = rms_norm(hidden, gain_row)
    queries = rotary(jnp.dot(normed, w_query, preferred_element_type=jnp.float32).reshape(batch_rows, -1, head_dim), positions)
    key_new = rotary(jnp.dot(normed, w_key, preferred_element_type=jnp.float32).reshape(batch_rows, kv_count, head_dim), positions)
    value_new = jnp.dot(normed, w_value, preferred_element_type=jnp.float32).reshape(batch_rows, kv_count, head_dim)
    slot_iota = lax.broadcasted_iota(jnp.int32, (batch_rows, k_cache.shape[1]), 1)
    slot_hit = (slot_iota == slot_ids[:, None])[:, :, None, None]
    k_cache = jnp.where(slot_hit, key_new.astype(jnp.bfloat16)[:, None], k_cache)
    v_cache = jnp.where(slot_hit, value_new.astype(jnp.bfloat16)[:, None], v_cache)
    grouped = queries.astype(jnp.bfloat16).reshape(batch_rows, kv_count, -1, head_dim)
    return grouped, k_cache, v_cache


def attention(grouped, k_cache, v_cache, key_valid):
    head_dim = grouped.shape[-1]
    logits = jnp.einsum('bgrd,bngd->bgrn', grouped, k_cache, preferred_element_type=jnp.float32) * head_dim ** -0.5
    logits = SOFT_CAP * jnp.tanh(logits / SOFT_CAP)
    if key_valid is not None:
        logits = jnp.where(key_valid[:, None, None, :], logits, NEG_FILL)
    attn_probs = jax.nn.softmax(logits, axis=-1).astype(jnp.bfloat16)
    mixed_heads = jnp.einsum('bgrn,bngd->bgrd', attn_probs, v_cache, preferred_element_type=jnp.float32)
    return mixed_heads.astype(jnp.bfloat16)


def mlp_part(normed, w_gate, w_up, w_down):
    gate_proj = jnp.dot(normed, w_gate, preferred_element_type=jnp.float32)
    up_proj = jnp.dot(normed, w_up, preferred_element_type=jnp.float32)
    hidden_act = (jax.nn.gelu(gate_proj, approximate=True) * up_proj).astype(jnp.bfloat16)
    return jnp.dot(hidden_act, w_down, preferred_element_type=jnp.float32)


def add_normed(hidden, branch_sum, gain_row):
    return (hidden.astype(jnp.float32) + rms_norm(branch_sum, gain_row).astype(jnp.float32)).astype(jnp.bfloat16)


def decoder_layer(hidden, positions, k_cache, v_cache, slot_ids, key_valid, layer_weights, gains):
    w_query, w_key, w_value, w_out, w_gate, w_up, w_down = layer_weights
    grouped, k_cache, v_cache = project_and_store(hidden, positions, k_cache, v_cache, slot_ids, w_query, w_key, w_value, gains[0])
    mixed_heads = attention(grouped, k_cache, v_cache, key_valid)
    attn_part = jnp.dot(mixed_heads.reshape(hidden.shape[0], -1), w_out, preferred_element_type=jnp.float32)
    attn_sum = lax.psum(attn_part.astype(jnp.bfloat16), 'tp')
    hidden = add_normed(hidden, attn_sum, gains[1])
    down_part = mlp_part(rms_norm(hidden, gains[2]), w_gate, w_up, w_down)
    down_sum = lax.psum(down_part.astype(jnp.bfloat16), 'tp')
    hidden = add_normed(hidden, down_sum, gains[3])
    return hidden, k_cache, v_cache


def decode_step(hidden, positions, k_local, v_local, k_global, v_global, w_query, w_key, w_value, w_out, w_gate, w_up, w_down, norm_scale):
    stacks = (w_query, w_key, w_value, w_out, w_gate, w_up, w_down)
    window = k_local.shape[1]
    global_valid = lax.broadcasted_iota(jnp.int32, (hidden.shape[0], k_global.shape[1]), 1) <= positions[:, None]
    hidden, k_local, v_local = decoder_layer(hidden, positions, k_local, v_local, positions % window, None, tuple(stacked[0] for stacked in stacks), norm_scale[0])
    hidden, k_global, v_global = decoder_layer(hidden, positions, k_global, v_global, positions, global_valid, tuple(stacked[1] for stacked in stacks), norm_scale[1])
    return hidden, k_local, v_local, k_global, v_global


def solution(mesh):
    row_spec = P('dp', None)
    cache_spec = P('dp', None, 'tp', None)
    col_split = P(None, None, 'tp')
    row_split = P(None, 'tp', None)
    in_specs = (row_spec, P('dp'), cache_spec, cache_spec, cache_spec, cache_spec, col_split, col_split, col_split, row_split, col_split, col_split, row_split, P())
    out_specs = (row_spec, cache_spec, cache_spec, cache_spec, cache_spec)
    return jax.shard_map(decode_step, mesh=mesh, in_specs=in_specs, out_specs=out_specs, check_vma=False)
```

profile of v0, /device:TPU:113, one launch (start us, length us, event | category | flops | bytes accessed | tf_op | source)
XLA Modules:
  0.0 192.4 jit_solution(15957752486721395864)
XLA Ops:
  0.7 1.0 fusion.128
  1.7 0.9 fusion.205
  2.6 0.1 iota_compare_fusion.2
  2.7 0.1 multiply_cosine_fusion.1
  2.8 0.9 iota_compare_fusion.1
  3.7 1.5 add_reduce_fusion
  5.2 1.9 %fusion.105 = bf16[3,256]{1,0:T(4,128)(2,1)S(1)} fusion(bf16[2,3840,256]{2,1,0:T(8,128)(2,1)} %param.22, bf16[3,3840]{1,0:T(4,128)(2,1)} %param.14, f32[3840]{0:T(1024)S(1)} %get-tuple-element.11, f32[3]{0:T(128)S(1)} %add_rsqrt_fusion.7), kind=kOutput, calls=%fused_computation.75 | convolution fusion | flops 5945088 | bytes 2013708 | tf_op jit(solution)/shard_map/dot_general | solution.py:37
  7.2 2.0 %fusion.93 = f32[3,1,256]{2,0,1:T(4,128)S(1)} fusion(bf16[2,3840,256]{2,1,0:T(8,128)(2,1)} %param.21, bf16[3,3840]{1,0:T(4,128)(2,1)} %param.14, f32[3840]{0:T(1024)S(1)} %get-tuple-element.11, f32[3]{0:T(128)S(1)} %add_rsqrt_fusion.7), kind=kOutput, calls=%fused_computation.71 | convolution fusion | flops 5944320 | bytes 2015244 | tf_op jit(solution)/shard_map/dot_general | solution.py:36
  9.2 0.2 fusion.188
  9.3 2.2 %broadcast_select_fusion.3 = (bf16[3,1024,1,256]{3,1,2,0:T(8,128)(2,1)S(1)}, bf16[3,1024,1,256]{3,1,2,0:T(8,128)(2,1)S(1)}) fusion(bf16[3,1024,1,256]{3,1,2,0:T(8,128)(2,1)} %param.16, pred[3,1024]{1,0:T(4,128)(4,1)S(1)} %iota_compare_fusion.2, bf16[3,256]{1,0:T(4,128)(2,1)S(1)} %pad_maximum_fusion.2, bf16[3,1024,1,256]{3,1,2,0:T(8,128)(2,1)} %param.17, ...), kind=kLoop, calls=%fused_computation.63 | loop fusion | flops 1572864 | bytes 6297600 | tf_op jit(solution)/shard_map/jit(_where)/select_n | solution.py:40
  11.5 0.0 copy-start.3
  11.5 3.5 %slice_bitcast_fusion = (bf16[512,3840]{0,1:T(8,128)(2,1)}, bf16[512,3840]{0,1:T(8,128)(2,1)}) fusion(bf16[2,3840,512]{2,1,0:T(8,128)(2,1)S(1)} %copy-done.2), kind=kLoop, calls=%fused_computation.39 | loop fusion | bytes 15728640 | tf_op jit(solution)/shard_map/dot_general | solution.py:35
  15.1 6.3 %copy.21 = bf16[512,3840]{1,0:T(8,128)(2,1)} copy(bf16[512,3840]{0,1:T(8,128)(2,1)} %get-tuple-element.19) | data formatting | bytes 7864320 | tf_op jit(solution)/shard_map/dot_general | solution.py:35
  21.3 6.3 %copy.19 = bf16[512,3840]{1,0:T(8,128)(2,1)} copy(bf16[512,3840]{0,1:T(8,128)(2,1)} %get-tuple-element.20) | data formatting | bytes 7864320 | tf_op jit(solution)/shard_map/dot_general | solution.py:35
  27.6 3.2 %fusion.164 = f32[3,2,256]{2,0,1:T(4,128)S(1)} fusion(bf16[2,256,3840]{2,1,0:T(8,128)(2,1)} %bitcast.140, bf16[3,3840]{1,0:T(4,128)(2,1)S(1)} %copy-done.5, f32[3840]{0:T(1024)S(1)} %get-tuple-element.11, f32[3]{0:T(128)S(1)} %add_rsqrt_fusion.7), kind=kOutput, calls=%fused_computation.147 | convolution fusion | flops 11842560 | bytes 3976716 | tf_op jit(solution)/shard_map/dot_general | solution.py:35
  30.9 0.5 fusion.84
  31.4 0.2 fusion.206
  31.6 0.4 fusion.99
  32.0 2.7 %convolution_convert_fusion.1 = bf16[3,3840]{1,0:T(4,128)(2,1)S(1)} fusion(bf16[3,512]{1,0:T(4,128)(2,1)S(1)} %bitcast.143, bf16[2,512,3840]{2,1,0:T(8,128)(2,1)} %param.23), kind=kOutput, calls=%fused_computation.35 | convolution fusion | flops 11808000 | bytes 3958272 | tf_op jit(solution)/shard_map/dot_general | solution.py:72
  34.7 24.0 %psum.28 = bf16[3,3840]{1,0:T(4,128)(2,1)S(1)} all-reduce(bf16[3,3840]{1,0:T(4,128)(2,1)S(1)} %convolution_convert_fusion.1), channel_id=1, replica_groups=mesh['dp'=2,'tp'=8] {'tp'}, use_global_device_ids=true, to_apply=%region_3.4 | all-reduce | flops 11520 | bytes 46080 | tf_op jit(solution)/shard_map/psum | solution.py:73
  58.7 0.1 fusion.116
  58.9 0.2 fusion.132
  59.1 6.4 %fusion.150 = f32[3,1920]{1,0:T(4,128)S(1)} fusion(bf16[2,3840,1920]{2,1,0:T(8,128)(2,1)} %param.24, bf16[3,3840]{1,0:T(4,128)(2,1)S(1)} %get-tuple-element.18, f32[3840]{0:T(1024)S(1)} %get-tuple-element.9, f32[3]{0:T(128)S(1)} %add_rsqrt_fusion.5), kind=kOutput, calls=%fused_computation.137 | convolution fusion | flops 44328960 | bytes 14807052 | tf_op jit(solution)/shard_map/dot_general | solution.py:58
  65.5 11.7 %fusion.38 = bf16[3,3840]{1,0:T(4,128)(2,1)S(1)} fusion(bf16[2,1920,3840]{2,1,0:T(8,128)(2,1)} %param.26, f32[3,1920]{1,0:T(4,128)S(1)} %fusion.150, bf16[2,3840,1920]{2,1,0:T(8,128)(2,1)} %param.25, bf16[3,3840]{1,0:T(4,128)(2,1)S(1)} %get-tuple-element.18, f32[3840]{0:T(1024)S(1)} %get-tuple-element.9, f32[3]{0:T(128)S(1)} %add_rsqrt_fusion.5), kind=kOutput, calls=%fused_computation.32 | convolution fusion | flops 88542720 | bytes 29575692 | tf_op jit(solution)/shard_map/dot_general | solution.py:61
  77.2 23.9 %psum.29 = bf16[3,3840]{1,0:T(4,128)(2,1)S(1)} all-reduce(bf16[3,3840]{1,0:T(4,128)(2,1)S(1)} %fusion.38), channel_id=1, replica_groups=mesh['dp'=2,'tp'=8] {'tp'}, use_global_device_ids=true, to_apply=%region_6.7 | all-reduce | flops 11520 | bytes 46080 | tf_op jit(solution)/shard_map/psum | solution.py:76
  101.1 0.1 fusion.119
  101.3 0.2 fusion.136
  101.5 3.2 %fusion.162 = f32[3,2,256]{2,0,1:T(4,128)S(1)} fusion(bf16[2,256,3840]{2,1,0:T(8,128)(2,1)} %bitcast.139, bf16[3,3840]{1,0:T(4,128)(2,1)S(1)} %get-tuple-element.16, f32[3840]{0:T(1024)S(1)} %get-tuple-element.7, f32[3]{0:T(128)S(1)} %add_rsqrt_fusion.3), kind=kOutput, calls=%fused_computation.145 | convolution fusion | flops 11842560 | bytes 3976716 | tf_op jit(solution)/shard_map/dot_general | solution.py:35
  104.7 1.9 fusion.108
  106.7 2.0 %fusion.96 = f32[3,1,256]{2,0,1:T(4,128)S(1)} fusion(bf16[2,3840,256]{2,1,0:T(8,128)(2,1)} %param.21, bf16[3,3840]{1,0:T(4,128)(2,1)S(1)} %get-tuple-element.16, f32[3840]{0:T(1024)S(1)} %get-tuple-element.7, f32[3]{0:T(128)S(1)} %add_rsqrt_fusion.3), kind=kOutput, calls=%fused_computation.72 | convolution fusion | flops 5944320 | bytes 2007564 | tf_op jit(solution)/shard_map/dot_general | solution.py:36
  108.6 0.2 fusion.186
  108.8 7.3 %broadcast_select_fusion.1 = (bf16[3,6144,1,256]{3,1,2,0:T(8,128)(2,1)S(1)}, bf16[3,6144,1,256]{3,1,2,0:T(8,128)(2,1)S(1)}) fusion(bf16[3,6144,1,256]{3,1,2,0:T(8,128)(2,1)} %param.18, pred[3,6144]{1,0:T(4,128)(4,1)S(1)} %get-tuple-element.36, bf16[3,256]{1,0:T(4,128)(2,1)S(1)} %pad_maximum_fusion.3, bf16[3,6144,1,256]{3,1,2,0:T(8,128)(2,1)} %param.19, ...), kind=kLoop, calls=%fused_computation.25 | loop fusion | flops 9437184 | bytes 37770240 | tf_op jit(solution)/shard_map/jit(_where)/select_n | solution.py:40
  116.1 0.0 slice-start
  116.2 2.5 %fusion.35 = f32[3,2,6144]{2,1,0:T(2,128)S(1)} fusion(bf16[3,6144,1,256]{3,1,2,0:T(8,128)(2,1)S(1)} %get-tuple-element.21, pred[3,6144]{1,0:T(4,128)(4,1)S(1)} %get-tuple-element.35, bf16[3,2,256]{2,0,1:T(4,128)(2,1)S(1)} %pad_maximum_fusion.1), kind=kOutput, calls=%fused_computation.31 | convolution fusion | flops 18984960 | bytes 9606144 | tf_op jit(solution)/shard_map/bgrd,bngd->bgrn/dot_general | solution.py:48
  118.7 0.3 fusion.207
  119.0 1.4 fusion.102
  120.4 0.5 copy-done
  120.9 4.0 %copy-done.1 = bf16[3,6144,1,256]{3,1,2,0:T(8,128)(2,1)} copy-done((bf16[3,6144,1,256]{3,1,2,0:T(8,128)(2,1)}, bf16[3,6144,1,256]{3,1,2,0:T(8,128)(2,1)S(1)}, u32[]{:S(2)}) %copy-start.1) | copy-done | bytes 9437208
  124.9 0.1 slice-done.1
  125.1 0.6 convolution_convert_fusion
  125.7 23.7 %psum.30 = bf16[3,3840]{1,0:T(4,128)(2,1)S(1)} all-reduce(bf16[3,3840]{1,0:T(4,128)(2,1)S(1)} %convolution_convert_fusion), channel_id=1, replica_groups=mesh['dp'=2,'tp'=8] {'tp'}, use_global_device_ids=true, to_apply=%region_11.12 | all-reduce | flops 11520 | bytes 46080 | tf_op jit(solution)/shard_map/psum | solution.py:73
  149.4 0.1 fusion.122
  149.5 0.2 fusion.140
  149.8 6.4 %fusion.159 = f32[3,1920]{1,0:T(4,128)S(1)} fusion(bf16[2,3840,1920]{2,1,0:T(8,128)(2,1)} %param.24, bf16[3,3840]{1,0:T(4,128)(2,1)S(1)} %get-tuple-element.14, f32[3840]{0:T(1024)S(1)} %get-tuple-element.12, f32[3]{0:T(128)S(1)} %add_rsqrt_fusion.1), kind=kOutput, calls=%fused_computation.144 | convolution fusion | flops 44328960 | bytes 14807052 | tf_op jit(solution)/shard_map/dot_general | solution.py:58
  156.1 11.7 %fusion.41 = bf16[3,3840]{1,0:T(4,128)(2,1)S(1)} fusion(bf16[2,1920,3840]{2,1,0:T(8,128)(2,1)} %param.26, f32[3,1920]{1,0:T(4,128)S(1)} %fusion.159, bf16[2,3840,1920]{2,1,0:T(8,128)(2,1)} %param.25, bf16[3,3840]{1,0:T(4,128)(2,1)S(1)} %get-tuple-element.14, f32[3840]{0:T(1024)S(1)} %get-tuple-element.12, f32[3]{0:T(128)S(1)} %add_rsqrt_fusion.1), kind=kOutput, calls=%fused_computation.33 | convolution fusion | flops 88542720 | bytes 29575692 | tf_op jit(solution)/shard_map/dot_general | solution.py:61
  167.9 23.7 %psum.31 = bf16[3,3840]{1,0:T(4,128)(2,1)S(1)} all-reduce(bf16[3,3840]{1,0:T(4,128)(2,1)S(1)} %fusion.41), channel_id=1, replica_groups=mesh['dp'=2,'tp'=8] {'tp'}, use_global_device_ids=true, to_apply=%region_14.15 | all-reduce | flops 11520 | bytes 46080 | tf_op jit(solution)/shard_map/psum | solution.py:76
  191.6 0.1 fusion.125
  191.7 0.7 fusion.143
  (29 shorter events, 0.2 us)
Async XLA Ops:
  0.6 10.9 %copy-start.2 = (bf16[2,3840,512]{2,1,0:T(8,128)(2,1)S(1)}, bf16[2,3840,512]{2,1,0:T(8,128)(2,1)}, u32[]{:S(2)}) copy-start(bf16[2,3840,512]{2,1,0:T(8,128)(2,1)} %param.20) | copy-start | bytes 23592964
  11.5 19.4 %copy-start.3 = (bf16[3,1024,1,256]{3,1,2,0:T(8,128)(2,1)}, bf16[3,1024,1,256]{3,1,2,0:T(8,128)(2,1)S(1)}, u32[]{:S(2)}) copy-start(bf16[3,1024,1,256]{3,1,2,0:T(8,128)(2,1)S(1)} %get-tuple-element.31) | copy-start | bytes 4718596
  11.5 20.1 %copy-start.4 = (bf16[3,1024,1,256]{3,1,2,0:T(8,128)(2,1)}, bf16[3,1024,1,256]{3,1,2,0:T(8,128)(2,1)S(1)}, u32[]{:S(2)}) copy-start(bf16[3,1024,1,256]{3,1,2,0:T(8,128)(2,1)S(1)} %get-tuple-element.32) | copy-start | bytes 4718596
  15.1 12.5 %copy-start.5 = (bf16[3,3840]{1,0:T(4,128)(2,1)S(1)}, bf16[3,3840]{1,0:T(4,128)(2,1)}, u32[]{:S(2)}) copy-start(bf16[3,3840]{1,0:T(4,128)(2,1)} %param.14) | copy-start | bytes 69124
  116.1 4.8 %copy-start = (bf16[3,6144,1,256]{3,1,2,0:T(8,128)(2,1)}, bf16[3,6144,1,256]{3,1,2,0:T(8,128)(2,1)S(1)}, u32[]{:S(2)}) copy-start(bf16[3,6144,1,256]{3,1,2,0:T(8,128)(2,1)S(1)} %get-tuple-element.21) | copy-start | bytes 28311556
  116.1 8.8 %copy-start.1 = (bf16[3,6144,1,256]{3,1,2,0:T(8,128)(2,1)}, bf16[3,6144,1,256]{3,1,2,0:T(8,128)(2,1)S(1)}, u32[]{:S(2)}) copy-start(bf16[3,6144,1,256]{3,1,2,0:T(8,128)(2,1)S(1)} %get-tuple-element.22) | copy-start | bytes 28311556
  116.1 8.8 %slice-start = ((s8[7864320]{0:T(1024)(128)(4,1)}), s8[4194304]{0:T(1024)(128)(4,1)S(1)}, s32[]{:S(2)}) async-start(s8[7864320]{0:T(1024)(128)(4,1)} %bitcast.141), calls=%async_computation | async-start | bytes 8388608
  116.1 8.9 %slice-start.1 = ((s8[7864320]{0:T(1024)(128)(4,1)}), s8[3670016]{0:T(1024)(128)(4,1)S(1)}, s32[]{:S(2)}) async-start(s8[7864320]{0:T(1024)(128)(4,1)} %bitcast.141), calls=%async_computation.1 | async-start | bytes 7340032
where the time goes:
time: 196 us; the launch traced here: 192 us
  blocking collectives  95.3 us (49%)
  matrix products  58.6 us (30%)
  local copies, waits for them, and re-layouts  20.7 us (11%)
  other arithmetic  17 us (9%)
    psum x2, blocking collectives, decoder_layer(): attn_sum = lax.psum(attn_part.astype(jnp.bfloat16), 'tp')  47.7 us
    psum x2, blocking collectives, decoder_layer(): down_sum = lax.psum(down_part.astype(jnp.bfloat16), 'tp')  47.6 us
    dot_general x2, matrix products, mlp_part(): return jnp.dot(hidden_act, w_down, preferred_element_type=jnp.float32)  23.4 us
    dot_general x3, local copies, waits for them, and re-layouts, project_and_store(): jnp.dot(normed, w_query, preferred_element_type=jnp.float32)  16.1 us
    dot_general x2, matrix products, mlp_part(): gate_proj = jnp.dot(normed, w_gate, preferred_element_type=jnp.float32)  12.7 us
    select_n x2, other arithmetic, project_and_store(): jnp.where(slot_hit, key_new.astype(jnp.bfloat16)[:, None], k_cache)  9.45 us
    dot_general x2, matrix products, project_and_store(): jnp.dot(normed, w_query, preferred_element_type=jnp.float32)  6.45 us
    unnamed x18, local copies, waits for them, and re-layouts  4.68 us

commit v1 on v0

v1 whole, which is shorter than its diff:
```python
import functools

import jax
import jax.numpy as jnp
from jax import lax
from jax.experimental import pallas as pl
from jax.experimental.pallas import tpu as pltpu
from jax.sharding import PartitionSpec as P

SOFT_CAP = 50.0
NORM_EPS = 1e-6
ROPE_BASE = 10000.0

TILE = 256
GATE_SLOTS = 10
GATE_BLOCK = 3
DOWN_SLOTS = 6
DOWN_COLS = 384
SEND_COLS = 768
QKV_ROWS = 768
SCORE_COLS = 1024
MESH = pl.DeviceIdType.MESH
F32 = jnp.float32
BF16 = jnp.bfloat16


def dot(lhs, rhs):
    return jnp.dot(lhs, rhs, preferred_element_type=F32)


def dot_t(lhs, rhs):
    return lax.dot_general(lhs, rhs, (((1,), (1,)), ((), ())), preferred_element_type=F32)


def pad_rows(top):
    return jnp.concatenate([top, jnp.zeros_like(top)], axis=0).astype(BF16)


def step_kernel(tp, hid, pos, kl, vl, kg, vg, wq, wk, wv, wo, wg, wu, wd, ns, out, klo, vlo, kgo, vgo, knew, vnew, hid_s, ns_s, qkv_s, wo_s, wg_s, wu_s, wd_s, x_s, a8_s, a16_s, acc_s, s_s, p_s, h_s, rb, m_sem, q_sem, c_sem, o_sem, g_sem, d_sem, s_sem, r_sem):
    rows, width = hid.shape
    head = kl.shape[-1]
    half = head // 2
    ff = wg.shape[-1]
    layers = wq.shape[0]
    q_cols = wq.shape[-1]
    windows = (kl.shape[1], kg.shape[1])
    n_gate = width // TILE
    n_down = width // DOWN_COLS
    n_send = width // SEND_COLS
    n_qkv = width // QKV_ROWS
    me = lax.axis_index('tp')

    barrier = pltpu.get_barrier_semaphore()
    for d in range(1, tp):
        pl.semaphore_signal(barrier, inc=1, device_id={'tp': lax.rem(me + d, tp)}, device_id_type=MESH)

    def qkv_copies(l, c):
        r = pl.ds(c * QKV_ROWS, QKV_ROWS)
        return [
            pltpu.make_async_copy(wq.at[l, r, :], qkv_s.at[r, pl.ds(0, q_cols)], q_sem.at[0, c]),
            pltpu.make_async_copy(wk.at[l, r, :], qkv_s.at[r, pl.ds(q_cols, head)], q_sem.at[1, c]),
            pltpu.make_async_copy(wv.at[l, r, :], qkv_s.at[r, pl.ds(q_cols + head, head)], q_sem.at[2, c]),
        ]

    def cache_copy(l, i, b):
        src = ((kl, vl), (kg, vg))[l][i]
        dst = ((klo, vlo), (kgo, vgo))[l][i]
        return pltpu.make_async_copy(src.at[b], dst.at[b], c_sem.at[l, i, b])

    def out_copy(l):
        return pltpu.make_async_copy(wo.at[l], wo_s, o_sem)

    def gate_copies(l, c):
        slot = c % GATE_SLOTS
        r = pl.ds(c * TILE, TILE)
        return [
            pltpu.make_async_copy(wg.at[l, r, :], wg_s.at[slot], g_sem.at[0, slot]),
            pltpu.make_async_copy(wu.at[l, r, :], wu_s.at[slot], g_sem.at[1, slot]),
        ]

    n_quad = n_down - DOWN_SLOTS

    def down_slot(j):
        if j < n_quad:
            return qkv_s.at[pl.ds((j // 2) * ff, ff), pl.ds((j % 2) * DOWN_COLS, DOWN_COLS)]
        return wd_s.at[j - n_quad]

    def down_copy(l, j):
        return pltpu.make_async_copy(wd.at[l, :, pl.ds(j * DOWN_COLS, DOWN_COLS)], down_slot(j), d_sem.at[j])

    hid_copy = pltpu.make_async_copy(hid, hid_s, m_sem.at[0])
    ns_copy = pltpu.make_async_copy(ns, ns_s, m_sem.at[1])
    hid_copy.start()
    ns_copy.start()
    for c in range(n_qkv):
        for cp in qkv_copies(0, c):
            cp.start()
    for i in range(2):
        for b in range(rows):
            cache_copy(0, i, b).start()
    out_copy(0).start()
    for c in range(GATE_SLOTS):
        for cp in gate_copies(0, c):
            cp.start()
    for b in range(rows - 1):
        cache_copy(1, 0, b).start()

    row8 = lax.broadcasted_iota(jnp.int32, (8, half), 0)
    pos8 = jnp.zeros((8, half), jnp.int32)
    for b in range(rows):
        pos8 = jnp.where(row8 == b, pos[b], pos8)
    lane = lax.broadcasted_iota(jnp.int32, (8, half), 1).astype(F32)
    angles = pos8.astype(F32) * jnp.exp(lane * (-2.0 / head * 9.210340371976184))
    cos_part = jnp.cos(angles)
    sin_part = jnp.sin(angles)

    def rotary(full):
        first, second = full[:, :half], full[:, half:]
        return jnp.concatenate([first * cos_part - second * sin_part, second * cos_part + first * sin_part], axis=-1)

    def blocks():
        return [slice(j * SEND_COLS, (j + 1) * SEND_COLS) for j in range(n_send)]

    def inv_rms(parts):
        total = sum(jnp.sum(p * p, axis=-1, keepdims=True) for p in parts)
        return lax.rsqrt(total * (1.0 / width) + NORM_EPS)

    def scaled(parts, l, i):
        inv = inv_rms(parts)
        return [(p * inv * (1.0 + ns_s[l, i : i + 1, cols])).astype(BF16) for p, cols in zip(parts, blocks())]

    def set_operand(parts):
        for p, cols in zip(parts, blocks()):
            a8_s[0:rows, cols] = p.astype(F32)
        for c in range(n_gate):
            cols = slice(c * TILE, (c + 1) * TILE)
            a16_s[:, cols] = pad_rows(a8_s[:, cols])

    def sends(ar, j):
        return [
            pltpu.make_async_remote_copy(
                src_ref=rb.at[ar, me, j],
                dst_ref=rb.at[ar, me, j],
                send_sem=s_sem.at[ar, d],
                recv_sem=r_sem.at[ar, me],
                device_id={'tp': lax.rem(me + d, tp)},
                device_id_type=MESH,
            )
            for d in range(1, tp)
        ]

    def whole(ar, d):
        src = lax.rem(me + d, tp)
        return pltpu.make_async_remote_copy(
            src_ref=rb.at[ar, src],
            dst_ref=rb.at[ar, src],
            send_sem=s_sem.at[ar, d],
            recv_sem=r_sem.at[ar, src],
            device_id={'tp': src},
            device_id_type=MESH,
        )

    def received(ar):
        for d in range(1, tp):
            whole(ar, d).wait_recv()
        parts = []
        for j in range(n_send):
            total = rb[ar, 0, j].astype(F32)
            for s in range(1, tp):
                total = total + rb[ar, s, j].astype(F32)
            parts.append(total)
        return parts

    def attend(l, q8, k8, v8):
        k_ref, v_ref = ((klo, vlo), (kgo, vgo))[l]
        n = windows[l]
        cols = min(SCORE_COLS, n)
        row16 = lax.broadcasted_iota(jnp.int32, (16, 1), 0)
        row16 = jnp.where(row16 >= 8, row16 - 8, row16)
        pos16 = jnp.zeros((16, 1), jnp.int32)
        for b in range(rows):
            pos16 = jnp.where(row16 == b, pos[b], pos16)
        slot16 = lax.rem(pos16, n) if l == 0 else pos16
        q16 = jnp.concatenate(q8, axis=0)
        s_new = jnp.concatenate([jnp.sum(q * k8, axis=-1, keepdims=True) for q in q8], axis=0)
        scale = head**-0.5 / SOFT_CAP

        def weight(s):
            return jnp.exp(SOFT_CAP * jnp.tanh(s * scale))

        q_row = [jnp.where(row16 == b, q16, 0.0).astype(BF16) for b in range(rows)]
        for b in range(rows):
            cache_copy(l, 0, b).wait()
            for t in range(n // cols):
                span = slice(t * cols, (t + 1) * cols)
                s = dot_t(q_row[b], k_ref[b, span, :])
                if b:
                    s = s + s_s[:, span]
                s_s[:, span] = s
        total = jnp.zeros((16, 1), F32)
        for t in range(n // cols):
            span = slice(t * cols, (t + 1) * cols)
            slot_ids = lax.broadcasted_iota(jnp.int32, (16, cols), 1) + t * cols
            e = weight(jnp.where(slot_ids == slot16, s_new, s_s[:, span]))
            if l:
                e = jnp.where(slot_ids <= pos16, e, 0.0)
            s_s[:, span] = e
            total = total + jnp.sum(e, axis=-1, keepdims=True)
        inv = 1.0 / total
        for t in range(n // cols):
            span = slice(t * cols, (t + 1) * cols)
            slot_ids = lax.broadcasted_iota(jnp.int32, (16, cols), 1) + t * cols
            p_s[:, span] = jnp.where(slot_ids == slot16, 0.0, s_s[:, span] * inv).astype(BF16)
        p_new = (weight(s_new) * inv).astype(BF16).astype(F32)
        mixed = p_new * jnp.concatenate([v8, v8], axis=0)
        for b in range(rows):
            cache_copy(l, 1, b).wait()
            mixed = mixed + jnp.where(row16 == b, dot(p_s[:, 0:n], v_ref[b]), 0.0)
        return jnp.concatenate([mixed[:8], mixed[8:]], axis=-1)

    a8_s[...] = jnp.zeros_like(a8_s)
    hid_copy.wait()
    ns_copy.wait()
    x = [hid_s[:, cols].astype(F32) for cols in blocks()]
    for l in range(layers):
        if l:
            x = [x_s[j] for j in range(n_send)]
        set_operand(scaled(x, l, 0))
        qkv = None
        for c in range(n_qkv):
            for cp in qkv_copies(l, c):
                cp.wait()
            r = slice(c * QKV_ROWS, (c + 1) * QKV_ROWS)
            part = dot(a16_s[:, r], qkv_s[r, :])[:8]
            qkv = part if qkv is None else qkv + part
        q8 = [rotary(qkv[:, h * head : (h + 1) * head]).astype(BF16).astype(F32) for h in range(q_cols // head)]
        k8 = rotary(qkv[:, q_cols : q_cols + head]).astype(BF16).astype(F32)
        v8 = qkv[:, q_cols + head : q_cols + 2 * head].astype(BF16).astype(F32)
        knew[l] = k8
        vnew[l] = v8
        mixed = pad_rows(attend(l, q8, k8, v8))

        out_copy(l).wait()
        ar = 2 * l
        if l == 0:
            pl.semaphore_wait(barrier, tp - 1)
        for j, cols in enumerate(blocks()):
            rb[ar, me, j] = dot(mixed, wo_s[:, cols])[:rows].astype(BF16)
            for cp in sends(ar, j):
                cp.start()
        if l == 0:
            x = [hid_s[:, cols].astype(F32) for cols in blocks()]
        else:
            x = [x_s[j] for j in range(n_send)]
        x = [(p + q.astype(F32)).astype(BF16).astype(F32) for p, q in zip(x, scaled(received(ar), l, 1))]
        for j in range(n_send):
            x_s[j] = x[j]
        set_operand(scaled(x, l, 2))

        for c0 in range(0, n_gate, GATE_BLOCK):
            chunks = range(c0, min(c0 + GATE_BLOCK, n_gate))
            for c in chunks:
                for cp in gate_copies(l, c):
                    cp.wait()
            for i, buf in enumerate((wg_s, wu_s)):
                part = sum(dot(a16_s[:, c * TILE : (c + 1) * TILE], buf[c % GATE_SLOTS]) for c in chunks)[:8]
                acc_s[i] = part if c0 == 0 else acc_s[i] + part
            for c in chunks:
                if c + GATE_SLOTS < n_gate:
                    for cp in gate_copies(l, c + GATE_SLOTS):
                        cp.start()
                if c + GATE_SLOTS == n_gate - 1:
                    for j in range(n_down):
                        down_copy(l, j).start()
                    if l == 0:
                        cache_copy(1, 0, rows - 1).start()
        h_s[...] = pad_rows(jax.nn.gelu(acc_s[0], approximate=True) * acc_s[1])

        ar = 2 * l + 1
        per_send = SEND_COLS // DOWN_COLS
        for j in range(n_send):
            chunks = range(j * per_send, (j + 1) * per_send)
            for c in chunks:
                down_copy(l, c).wait()
            for i, c in enumerate(chunks):
                rb[ar, me, j, :, i * DOWN_COLS : (i + 1) * DOWN_COLS] = dot(h_s[...], down_slot(c)[...])[:rows].astype(BF16)
            for cp in sends(ar, j):
                cp.start()
            if l == 0 and (j + 1) * per_send == n_quad:
                for c in range(n_qkv):
                    for cp in qkv_copies(1, c):
                        cp.start()
                for b in range(rows):
                    cache_copy(1, 1, b).start()
                out_copy(1).start()
                for c in range(GATE_SLOTS):
                    for cp in gate_copies(1, c):
                        cp.start()
        x = [x_s[j] for j in range(n_send)]
        x = [(p + q.astype(F32)).astype(BF16) for p, q in zip(x, scaled(received(ar), l, 3))]
        if l + 1 < layers:
            for j in range(n_send):
                x_s[j] = x[j].astype(F32)
        else:
            for j, cols in enumerate(blocks()):
                out[:, cols] = x[j]
    for ar in range(2 * layers):
        for d in range(1, tp):
            whole(ar, d).wait_send()


def store_kernel(pos, knew, vnew, kl, vl, kg, vg, klo, vlo, kgo, vgo, kl_s, vl_s, kg_s, vg_s, sem):
    rows = kl.shape[0]
    copies = []
    for l, (k_ref, v_ref, k_out, v_out) in enumerate(((kl_s, vl_s, klo, vlo), (kg_s, vg_s, kgo, vgo))):
        window = k_ref.shape[1]
        for i, (new, ref, dst) in enumerate(((knew, k_ref, k_out), (vnew, v_ref, v_out))):
            for b in range(rows):
                slot = lax.rem(pos[b], window)
                base = pl.multiple_of((slot // 16) * 16, 16)
                tile = ref[b, pl.ds(base, 16), :].astype(F32)
                hit = lax.broadcasted_iota(jnp.int32, tile.shape, 0) == slot - base
                ref[b, pl.ds(base, 16), :] = jnp.where(hit, new[l, b : b + 1, :], tile).astype(BF16)
                cp = pltpu.make_async_copy(ref.at[b], dst.at[b], sem.at[l, i, b])
                cp.start()
                copies.append(cp)
    for cp in copies:
        cp.wait()


def decode_step(tp, hidden, positions, k_local, v_local, k_global, v_global, w_query, w_key, w_value, w_out, w_gate, w_up, w_down, norm_scale):
    rows, width = hidden.shape
    head = k_local.shape[-1]
    layers = w_query.shape[0]
    ff = w_gate.shape[-1]
    caches = [c.reshape(rows, c.shape[1], head) for c in (k_local, v_local, k_global, v_global)]
    window = k_global.shape[1]
    hbm = lambda v: pltpu.with_memory_space_constraint(v, pltpu.HBM)
    any_spec = pl.BlockSpec(memory_space=pl.ANY)
    vmem_spec = pl.BlockSpec(memory_space=pltpu.VMEM)
    smem_spec = pl.BlockSpec(memory_space=pltpu.SMEM)
    dma = pltpu.SemaphoreType.DMA
    n_send = width // SEND_COLS
    big = [hbm(v) for v in (*caches, w_query, w_key, w_value, w_out, w_gate, w_up, w_down)]
    cache_shapes = [pltpu.VMEM(c.shape, BF16) for c in caches]
    new_shape = pltpu.VMEM((layers, 8, head), F32)
    out, klo, vlo, kgo, vgo, knew, vnew = pl.pallas_call(
        functools.partial(step_kernel, tp),
        out_shape=(jax.ShapeDtypeStruct((rows, width), BF16), *cache_shapes, new_shape, new_shape),
        in_specs=[any_spec, smem_spec] + [any_spec] * 12,
        out_specs=(vmem_spec,) * 7,
        scratch_shapes=[
            pltpu.VMEM((rows, width), BF16),
            pltpu.VMEM(norm_scale.shape, F32),
            pltpu.VMEM((width, w_query.shape[-1] + 2 * head), BF16),
            pltpu.VMEM(w_out.shape[1:], BF16),
            pltpu.VMEM((GATE_SLOTS, TILE, ff), BF16),
            pltpu.VMEM((GATE_SLOTS, TILE, ff), BF16),
            pltpu.VMEM((DOWN_SLOTS, ff, DOWN_COLS), BF16),
            pltpu.VMEM((n_send, rows, SEND_COLS), F32),
            pltpu.VMEM((8, width), F32),
            pltpu.VMEM((16, width), BF16),
            pltpu.VMEM((2, 8, ff), F32),
            pltpu.VMEM((16, window), F32),
            pltpu.VMEM((16, window), BF16),
            pltpu.VMEM((16, ff), BF16),
            pltpu.VMEM((2 * layers, tp, n_send, rows, SEND_COLS), BF16),
            dma((2,)),
            dma((3, width // QKV_ROWS)),
            dma((2, 2, rows)),
            dma(()),
            dma((2, GATE_SLOTS)),
            dma((width // DOWN_COLS,)),
            dma((2 * layers, tp)),
            dma((2 * layers, tp)),
        ],
        compiler_params=pltpu.CompilerParams(vmem_limit_bytes=42 * 2**20, collective_id=0, has_side_effects=True),
        name='decode',
    )(hbm(hidden), positions, *big, hbm(norm_scale))
    stored = pl.pallas_call(
        store_kernel,
        out_shape=tuple(jax.ShapeDtypeStruct(c.shape, BF16) for c in caches) + tuple(cache_shapes),
        in_specs=[smem_spec] + [vmem_spec] * 6,
        out_specs=(any_spec,) * 4 + (vmem_spec,) * 4,
        input_output_aliases={3: 4, 4: 5, 5: 6, 6: 7},
        scratch_shapes=[dma((2, 2, rows))],
        compiler_params=pltpu.CompilerParams(vmem_limit_bytes=2 * 2**20),
        name='store',
    )(positions, knew, vnew, klo, vlo, kgo, vgo)
    return (out, *(s.reshape(c.shape) for s, c in zip(stored[:4], (k_local, v_local, k_global, v_global))))


def solution(mesh):
    row_spec = P('dp', None)
    cache_spec = P('dp', None, 'tp', None)
    col_split = P(None, None, 'tp')
    row_split = P(None, 'tp', None)
    in_specs = (row_spec, P('dp'), cache_spec, cache_spec, cache_spec, cache_spec, col_split, col_split, col_split, row_split, col_split, col_split, row_split, P())
    out_specs = (row_spec, cache_spec, cache_spec, cache_spec, cache_spec)
    return jax.shard_map(functools.partial(decode_step, mesh.shape['tp']), mesh=mesh, in_specs=in_specs, out_specs=out_specs, check_vma=False)
```

time: 196 us -> 83.7 us (0.43); the launches traced: 192 us -> 83.6 us
  blocking collectives: 95.3 us -> 0 us
  Pallas kernels: 0 us -> 82.3 us
  matrix products: 58.6 us -> 0 us
  local copies, waits for them, and re-layouts: 20.7 us -> 0.62 us
  other arithmetic: 17 us -> 0 us
    psum x4 -> x0, blocking collectives: 95.3 us -> none  [the longest x2 47.7 us: decoder_layer(): attn_sum = lax.psum(attn_part.astype(jnp.bfloat16), 'tp')]
    pallas_call x0 -> x2, Pallas kernels: none -> 82.3 us  [the longest x1 74.1 us: decode_step(): pl.pallas_call(functools.partial(step_kernel, tp), out_shape=(jax.ShapeDt...]
    dot_general x16 -> x0, matrix products: 58.6 us -> none  [the longest x2 23.4 us: mlp_part(): return jnp.dot(hidden_act, w_down, preferred_element_type=jnp.float32)]
    dot_general x3 -> x0, local copies, waits for them, and re-layouts: 16.1 us -> none  [project_and_store(): jnp.dot(normed, w_query, preferred_element_type=jnp.float32)]
    select_n x2 -> x0, other arithmetic: 9.45 us -> none  [project_and_store(): jnp.where(slot_hit, key_new.astype(jnp.bfloat16)[:, None], k_cache)]
    unnamed x18 -> x5, local copies, waits for them, and re-layouts: 4.68 us -> 0.62 us
    reduce_sum x8 -> x0, other arithmetic: 2.29 us -> none  [rms_norm(): jnp.mean(values_f32 * values_f32, axis=-1, keepdims=True) + NORM_EPS]
where the time goes in v1:
time: 83.7 us; the launch traced here: 83.6 us
  Pallas kernels  82.3 us (98%)
    pallas_call x1, Pallas kernels, decode_step(): pl.pallas_call(functools.partial(step_kernel, tp), out_shape=(jax.ShapeDt...  74.1 us
    pallas_call x1, Pallas kernels, decode_step(): pl.pallas_call(store_kernel, out_shape=tuple((jax.ShapeDtypeStruct(c.shap...  8.18 us

profile of v1, /device:TPU:113, one launch (start us, length us, event | category | flops | bytes accessed | tf_op | source)
XLA Modules:
  0.0 83.6 jit_solution(2685693050889263398)
XLA Ops:
  0.6 0.0 copy-start
  0.6 74.1 %decode.1 = (bf16[3,3840]{1,0:T(4,128)(2,1)}, bf16[3,1024,256]{2,1,0:T(8,128)(2,1)S(1)}, bf16[3,1024,256]{2,1,0:T(8,128)(2,1)S(1)}, bf16[3,6144,256]{2,1,0:T(8,1...) custom-call(bf16[3,3840]{1,0:T(4,128)(2,1)} %hid.1, s32[3]{0:T(128)} %pos.3, ...), custom_call_target="tpu_custom_call" | custom-call | tf_op jit(solution)/shard_map/decode/pallas_call | solution.py:347
  74.8 0.0 copy-done
  74.8 0.0 copy-start.1
  74.8 8.2 %store.1 = (bf16[3,1024,256]{2,1,0:T(8,128)(2,1)}, bf16[3,1024,256]{2,1,0:T(8,128)(2,1)}, bf16[3,6144,256]{2,1,0:T(8,128)(2,1)}, bf16[3,6144,256]{2,1,0:T(8,128)...) custom-call(s32[3]{0:T(128)S(1)} %copy-done, ...), custom_call_target="tpu_custom_call", output_to_operand_aliasing={{4}: (3, {}), {5}: (4, {}), {6}: (5, {}), {7}: (6, {})} | custom-call | tf_op jit(solution)/shard_map/store/pallas_call | solution.py:380
  83.0 0.0 copy-done.1
  83.0 0.6 copy.32
Async XLA Ops:
  0.6 74.1 %copy-start = (s32[3]{0:T(128)S(1)}, s32[3]{0:T(128)}, u32[]{:S(2)}) copy-start(s32[3]{0:T(128)} %pos.3) | copy-start | bytes 40
  74.8 8.2 %copy-start.1 = (bf16[3,3840]{1,0:T(4,128)(2,1)S(1)}, bf16[3,3840]{1,0:T(4,128)(2,1)}, u32[]{:S(2)}) copy-start(bf16[3,3840]{1,0:T(4,128)(2,1)} %get-tuple-element.37) | copy-start | bytes 69124
